TPU v7x, 128 devices: a whole 4x4x4 slice. The times are simulated.
128 devices in a mesh: row: 8 (over y, z_lo), col: 16 (over x, z_hi, core).
Axes of the slice: x: 4, y: 4, z: 4 (z_hi: 2, z_lo: 2; z = z_hi * 2 + z_lo), core: 2. Of those that a mesh axis runs over, the one named last changes fastest.
Arguments:
- hidden_states: bfloat16 [16384, 8192], P(('row', 'col')), may hold values from -6 to 6
- w_c: bfloat16 [8192, 512], replicated, may hold values from -0.0625 to 0.0625
- w_b: bfloat16 [8192, 128], replicated, may hold values from -0.0625 to 0.0625
- teacher_q: bfloat16 [16384, 512], P(('row', 'col')), may hold values from -4 to 4
- teacher_k: bfloat16 [16384, 128], P(('row', 'col')), may hold values from -4 to 4
Outputs:
- grad_c: bfloat16 [16384, 512], P(('row', 'col'))
- grad_b: bfloat16 [16384, 128], P(('row', 'col'))
All inputs are finite; a program needn't handle non-finite values.
Results may differ from a plain program's by a relative error of at most 0.0056.
Values may be sent and summed in bfloat16 or wider, within the bound.
No kernel may reach another device: no remote copies, remote signals or barrier semaphores. Data moves between devices by JAX's collectives and lax.ppermute only.
A program may use at most 128 MiB of HBM per device.

v0:
```python
import math
import jax
import jax.numpy as jnp
from jax import lax
from jax.sharding import PartitionSpec as P

HEADS = 4
HEAD = 128
TOK_DEV = 128
LOSS_GAIN = 16.0
LENGTH_BASE = 512.0
NEGATIVE = -1e30


def teacher_logits(query_rows, key_rows, query_pos, key_pos):
    count = query_rows.shape[0]
    shaped = query_rows.reshape(count, HEADS, HEAD)
    logits = jnp.einsum("qhp,kp->hqk", shaped, key_rows, preferred_element_type=jnp.float32)
    temper = jnp.log(query_pos.astype(jnp.float32) + 2.0) / (
        math.log(LENGTH_BASE) * math.sqrt(HEAD)
    )
    logits = logits * temper[None, :, None]
    visible = key_pos[None, None, :] <= query_pos[None, :, None]
    return (jnp.where(visible, logits, NEGATIVE), visible)


def error_terms(logits, visible, peak, total, c_rows, b_rows, query_pos):
    probs = jnp.where(visible, jnp.exp(logits - peak[:, :, None]), 0.0) / total[:, :, None]
    count = c_rows.shape[0]
    shaped = c_rows.reshape(count, HEADS, HEAD)
    student = jnp.einsum("qhp,kp->hqk", shaped, b_rows, preferred_element_type=jnp.float32)
    student = student / (math.sqrt(HEAD) * (query_pos.astype(jnp.float32) + 1.0))[None, :, None]
    error = jnp.where(visible, student - probs, 0.0).astype(jnp.bfloat16)
    row_part = jnp.einsum("hqk,kp->qhp", error, b_rows, preferred_element_type=jnp.float32)
    key_part = jnp.einsum("hqk,qhp->kp", error, shaped, preferred_element_type=jnp.float32)
    return (row_part.reshape(count, HEADS * HEAD), key_part)


def on_device(hidden_states, w_c, w_b, teacher_q, teacher_k):
    c_proj = jnp.dot(hidden_states, w_c, preferred_element_type=jnp.float32).astype(jnp.bfloat16)
    b_proj = jnp.dot(hidden_states, w_b, preferred_element_type=jnp.float32).astype(jnp.bfloat16)
    key_rows, b_rows = (
        lax.all_gather(teacher_k, ("row", "col"), axis=0, tiled=True),
        lax.all_gather(b_proj, ("row", "col"), axis=0, tiled=True),
    )
    total_keys = key_rows.shape[0]
    width = math.gcd(2048, total_keys)
    turns = total_keys // width
    position_base = (lax.axis_index("row") * lax.axis_size("col") + lax.axis_index("col")) * TOK_DEV
    query_pos = position_base + jnp.arange(TOK_DEV, dtype=jnp.int32)
    key_split = key_rows.reshape(turns, width, HEAD)
    b_split = b_rows.reshape(turns, width, HEAD)
    pos_split = jnp.arange(total_keys, dtype=jnp.int32).reshape(turns, width)

    def stats_step(carry, pieces):
        logits, visible = teacher_logits(teacher_q, pieces[0], query_pos, pieces[1])
        newest = jnp.maximum(carry[0], jnp.max(logits, axis=2))
        summed = jnp.sum(jnp.where(visible, jnp.exp(logits - newest[:, :, None]), 0.0), axis=2)
        return ((newest, carry[1] * jnp.exp(carry[0] - newest) + summed), None)

    start_stats = (
        jnp.full((HEADS, TOK_DEV), NEGATIVE, jnp.float32),
        jnp.zeros((HEADS, TOK_DEV), jnp.float32),
    )
    (peak, total), unused = lax.scan(stats_step, start_stats, (key_split, pos_split))

    def rows_step(running, pieces):
        logits, visible = teacher_logits(teacher_q, pieces[0], query_pos, pieces[2])
        row_part, key_part = error_terms(logits, visible, peak, total, c_proj, pieces[1], query_pos)
        return (running + row_part, key_part)

    grad_rows, key_stack = lax.scan(
        rows_step, jnp.zeros((TOK_DEV, HEADS * HEAD), jnp.float32), (key_split, b_split, pos_split)
    )
    grad_keys = lax.psum_scatter(
        key_stack.reshape(total_keys, HEAD), ("row", "col"), scatter_dimension=0, tiled=True
    )
    factor = LOSS_GAIN / math.sqrt(HEAD)
    return ((grad_rows * factor).astype(jnp.bfloat16), (grad_keys * factor).astype(jnp.bfloat16))


def solution(mesh):
    return jax.shard_map(
        on_device,
        mesh=mesh,
        in_specs=(
            P(("row", "col"), None),
            P(),
            P(),
            P(("row", "col"), None),
            P(("row", "col"), None),
        ),
        out_specs=(P(("row", "col"), None), P(("row", "col"), None)),
        check_vma=False,
    )
```

profile of v0, /device:TPU:0, one launch (start us, length us, event | category | flops | bytes accessed | tf_op | source)
XLA Modules:
  0.0 1143.7 jit_solution(9247274924135349239)
XLA Ops:
  8.8 2.9 convolution_convert_fusion.1
  11.8 4.7 convolution_convert_fusion
  16.5 193.4 %all-gather.5.cloned.1.call-done = bf16[16384,128]{1,0:T(8,128)(2,1)} async-done(((bf16[128,128]{1,0:T(8,128)(2,1)}), bf16[16384,128]{1,0:T(8,128)(2,1)}) %all-gather.5.cloned.1.call-update) | async-done | bytes 4194320 | tf_op jit(solution)/shard_map/all_gather | solution.py:43
  210.0 58.9 %while.33 = (s32[]{:T(128)}, f32[4,128]{1,0:T(4,128)S(1)}, f32[4,128]{1,0:T(4,128)S(1)}, s32[8,2048]{1,0:T(8,128)S(1)}, bf16[8,2048,128]{2,1,0:T(8,128)(2,1)}, /...) while((s32[]{:T(128)}, f32[4,128]{1,0:T(4,128)S(1)}, ...), condition=%wide.region_3.4_spmd.clone.clone.clone, body=%wide.region_0.3_spmd.clone.clone.clone.sunk | while | flops 277089408 | bytes 9884788 | solution.py:65
  210.3 3.7 fusion.81
  214.0 3.2 select_reduce_fusion.2
  217.7 3.7 fusion.81
  221.4 3.2 select_reduce_fusion.2
  225.1 3.7 fusion.81
  228.8 3.2 select_reduce_fusion.2
  232.4 3.7 fusion.81
  236.2 3.2 select_reduce_fusion.2
  239.8 3.7 fusion.81
  243.5 3.2 select_reduce_fusion.2
  247.2 3.7 fusion.81
  250.9 3.2 select_reduce_fusion.2
  254.5 3.7 fusion.81
  258.2 3.2 select_reduce_fusion.2
  261.9 3.7 fusion.81
  265.6 3.2 select_reduce_fusion.2
  268.9 139.5 %all-gather.3.cloned.1.call-done = bf16[16384,128]{1,0:T(8,128)(2,1)} async-done(((bf16[128,128]{1,0:T(8,128)(2,1)}), bf16[16384,128]{1,0:T(8,128)(2,1)}) %all-gather.3.cloned.1.call-update) | async-done | bytes 4194320 | tf_op jit(solution)/shard_map/all_gather | solution.py:44
  408.3 66.1 %while.34 = (s32[]{:T(128)}, f32[128,512]{0,1:T(8,128)S(1)}, f32[8,2048,128]{2,1,0:T(8,128)}, bf16[8,2048,128]{2,1,0:T(8,128)(2,1)}, s32[8,2048]{1,0:T(8,128)S(1...) while((s32[]{:T(128)}, f32[128,512]{0,1:T(8,128)S(1)}, ...), condition=%wide.region_5.6_spmd.clone.clone.clone, body=%wide.region_4.5_spmd.clone.clone.clone.sunk | while | flops 1083573120 | bytes 19301524 | solution.py:72
  410.5 2.8 fusion.96
  418.7 2.8 fusion.96
  421.5 1.8 fusion.98
  427.0 2.8 fusion.96
  435.3 2.8 fusion.96
  443.5 2.8 fusion.96
  451.8 2.8 fusion.96
  460.0 2.8 fusion.96
  468.3 2.8 fusion.96
  475.2 660.4 %reduce-scatter.2.cloned.1.call-done = f32[128,128]{1,0:T(8,128)} async-done(((f32[16384,128]{1,0:T(8,128)}), f32[128,128]{1,0:T(8,128)}) %reduce-scatter.2.cloned.1.call-update) | async-done | bytes 65552 | tf_op jit(solution)/shard_map/reduce_scatter | solution.py:75
  (137 shorter events, 48.4 us)
Async XLA Ops:
  7.2 1.6 copy-start
  7.2 202.8 %all-gather.5.cloned.1.call-start = ((), (), s32[]{:S(2)}) async-start(), calls=%async_computation.2 | async-start | bytes 4227072 | tf_op jit(solution)/shard_map/all_gather | solution.py:43
  7.9 400.4 %all-gather.3.cloned.1.call-start = ((), (), s32[]{:S(2)}) async-start(), calls=%async_computation.1 | async-start | bytes 4227072 | tf_op jit(solution)/shard_map/all_gather | solution.py:44
  11.7 1124.0 %reduce-scatter.2.cloned.1.call-start = ((), (), s32[]{:S(2)}) async-start(), calls=%async_computation.3 | async-start | bytes 8454144 | tf_op jit(solution)/shard_map/reduce_scatter | solution.py:75
  11.8 198.2 %copy-start.1 = (bf16[128,512]{1,0:T(8,128)(2,1)S(1)}, bf16[128,512]{1,0:T(8,128)(2,1)}, u32[]{:S(2)}) copy-start(bf16[128,512]{1,0:T(8,128)(2,1)} %param.12) | copy-start | bytes 393220
Sparse Core Ops, SparseCore 0:
  9.7 200.2 all-gather.4
  212.3 196.0 all-gather.2
  474.6 661.0 reduce-scatter.1
where the time goes:
time: 1150 us; the launch traced here: 1140 us
  waiting for transfers between devices  994 us (86%)
  matrix products  99.3 us (9%)
  other arithmetic  34.2 us (3%)
  between operations  13.8 us (1%)
    reduce_scatter x1, waiting for transfers between devices, on_device(): lax.psum_scatter(key_stack.reshape(total_keys, HEAD), ('row', 'col'), sca...  660 us
    all_gather x1, waiting for transfers between devices, on_device(): lax.all_gather(teacher_k, ('row', 'col'), axis=0, tiled=True)  193 us
    all_gather x1, waiting for transfers between devices, on_device(): lax.all_gather(b_proj, ('row', 'col'), axis=0, tiled=True)  139 us
    dot_general x16, matrix products, teacher_logits(): jnp.einsum('qhp,kp->hqk', shaped, key_rows, preferred_element_type=jnp.fl...  51.9 us
    reduce_sum x8, other arithmetic, stats_step(): jnp.sum(jnp.where(visible, jnp.exp(logits - newest[:, :, None]), 0.0), ax...  25.8 us
  transfers between devices with their start and end apart: 3, of which 3 were waited for; matrix products, arithmetic and copies ran while one was open for 6% of the time, Pallas kernels for 0%

commit v1 on v0

--- a/solution.py
+++ b/solution.py
@@ -40,7 +40,12 @@
     c_proj = jnp.dot(hidden_states, w_c, preferred_element_type=jnp.float32).astype(jnp.bfloat16)
     b_proj = jnp.dot(hidden_states, w_b, preferred_element_type=jnp.float32).astype(jnp.bfloat16)
     key_rows, b_rows = (
-        lax.all_gather(teacher_k, ("row", "col"), axis=0, tiled=True),
+        jnp.concatenate(
+            lax.all_to_all(
+                jnp.stack([teacher_k] * lax.axis_size(("row", "col"))), ("row", "col"), 0, 0
+            ),
+            axis=0,
+        ),
         lax.all_gather(b_proj, ("row", "col"), axis=0, tiled=True),
     )
     total_keys = key_rows.shape[0]

time: 1150 us -> 986 us (0.86)
  waiting for transfers between devices: 994 us -> 819 us
  starting transfers between devices: 0.12 us -> 11.8 us
    all_gather x1 -> x0, waiting for transfers between devices: 193 us -> none  [on_device(): lax.all_gather(teacher_k, ('row', 'col'), axis=0, tiled=True)]
    all_to_all x0 -> x1, waiting for transfers between devices: none -> 45 us  [on_device(): lax.all_to_all(jnp.stack([teacher_k] * lax.axis_size(('row', 'col'))), ('...]
    all_gather x1, waiting for transfers between devices: 139 us -> 112 us  [on_device(): lax.all_gather(b_proj, ('row', 'col'), axis=0, tiled=True)]
    all_to_all x0 -> x1, starting transfers between devices: none -> 11.7 us  [on_device(): lax.all_to_all(jnp.stack([teacher_k] * lax.axis_size(('row', 'col'))), ('...]
  transfers between devices with their start and end apart: 3 -> 3, of which waited for: 3 -> 3; matrix products, arithmetic and copies ran while one was open for 6% -> 7% of each run, Pallas kernels for 0% -> 0%
where the time goes in v1:
time: 986 us; the launch traced here: 984 us
  waiting for transfers between devices  819 us (83%)
  matrix products  99.2 us (10%)
  other arithmetic  34.2 us (3%)
  between operations  14.1 us (1%)
  starting transfers between devices  11.8 us (1%)
    reduce_scatter x1, waiting for transfers between devices, on_device(): lax.psum_scatter(key_stack.reshape(total_keys, HEAD), ('row', 'col'), sca...  662 us
    all_gather x1, waiting for transfers between devices, on_device(): lax.all_gather(b_proj, ('row', 'col'), axis=0, tiled=True)  112 us
    dot_general x16, matrix products, teacher_logits(): jnp.einsum('qhp,kp->hqk', shaped, key_rows, preferred_element_type=jnp.fl...  51.8 us
    all_to_all x1, waiting for transfers between devices, on_device(): lax.all_to_all(jnp.stack([teacher_k] * lax.axis_size(('row', 'col'))), ('...  45 us
    reduce_sum x8, other arithmetic, stats_step(): jnp.sum(jnp.where(visible, jnp.exp(logits - newest[:, :, None]), 0.0), ax...  25.8 us
  transfers between devices with their start and end apart: 3, of which 3 were waited for; matrix products, arithmetic and copies ran while one was open for 7% of the time, Pallas kernels for 0%

profile of v1, /device:TPU:0, one launch (start us, length us, event | category | flops | bytes accessed | tf_op | source)
XLA Modules:
  0.0 983.8 jit_solution(18238604275300601476)
XLA Ops:
  7.2 3.9 stack.2
  11.1 11.7 %all-to-all-start = ((bf16[128,128,128]{2,1,0:T(8,128)(2,1)}), bf16[128,128,128]{2,1,0:T(8,128)(2,1)}, u32[]{:S(2)}, u32[]{:S(2)}) async-start(bf16[128,128,128]{2,1,0:T(8,128)(2,1)} %stack.2), calls=%async_computation | async-start | bytes 8388608 | tf_op jit(solution)/shard_map/all_to_all | solution.py:44
  22.8 2.9 convolution_convert_fusion.1
  25.9 4.7 convolution_convert_fusion
  30.6 45.0 %all-to-all-done = bf16[128,128,128]{2,1,0:T(8,128)(2,1)} async-done(((bf16[128,128,128]{2,1,0:T(8,128)(2,1)}), bf16[128,128,128]{2,1,0:T(8,128)(2,1)}, u32[]{:S(2)}, u32[]{:S(2)}) %all-to-all-start) | async-done | bytes 4194336 | tf_op jit(solution)/shard_map/all_to_all | solution.py:44
  75.6 58.8 %while.33 = (s32[]{:T(128)}, f32[4,128]{1,0:T(4,128)S(1)}, f32[4,128]{1,0:T(4,128)S(1)}, s32[8,2048]{1,0:T(8,128)S(1)}, bf16[8,2048,128]{2,1,0:T(8,128)(2,1)}, /...) while((s32[]{:T(128)}, f32[4,128]{1,0:T(4,128)S(1)}, ...), condition=%wide.region_3.4_spmd.clone.clone.clone, body=%wide.region_0.3_spmd.clone.clone.clone.sunk | while | flops 277089408 | bytes 9884788 | solution.py:70
  76.0 3.7 fusion.81
  79.7 3.2 select_reduce_fusion.2
  83.4 3.7 fusion.81
  87.1 3.2 select_reduce_fusion.2
  90.7 3.7 fusion.81
  94.4 3.2 select_reduce_fusion.2
  98.1 3.7 fusion.81
  101.8 3.2 select_reduce_fusion.2
  105.4 3.7 fusion.81
  109.1 3.2 select_reduce_fusion.2
  112.8 3.7 fusion.81
  116.5 3.2 select_reduce_fusion.2
  120.1 3.7 fusion.81
  123.8 3.2 select_reduce_fusion.2
  127.5 3.7 fusion.81
  131.2 3.2 select_reduce_fusion.2
  134.5 112.2 %all-gather.2.cloned.1.call-done = bf16[16384,128]{1,0:T(8,128)(2,1)} async-done(((bf16[128,128]{1,0:T(8,128)(2,1)}), bf16[16384,128]{1,0:T(8,128)(2,1)}) %all-gather.2.cloned.1.call-update) | async-done | bytes 4194320 | tf_op jit(solution)/shard_map/all_gather | solution.py:49
  246.6 66.0 %while.34 = (s32[]{:T(128)}, f32[128,512]{0,1:T(8,128)S(1)}, f32[8,2048,128]{2,1,0:T(8,128)}, bf16[8,2048,128]{2,1,0:T(8,128)(2,1)}, s32[8,2048]{1,0:T(8,128)S(1...) while((s32[]{:T(128)}, f32[128,512]{0,1:T(8,128)S(1)}, ...), condition=%wide.region_5.6_spmd.clone.clone.clone, body=%wide.region_4.5_spmd.clone.clone.clone.sunk | while | flops 1083573120 | bytes 19301524 | solution.py:77
  248.8 2.8 fusion.96
  257.0 2.8 fusion.96
  265.3 2.8 fusion.96
  273.5 2.8 fusion.96
  281.8 2.8 fusion.96
  290.0 2.8 fusion.96
  298.3 2.8 fusion.96
  313.5 662.0 %reduce-scatter.2.cloned.1.call-done = f32[128,128]{1,0:T(8,128)} async-done(((f32[16384,128]{1,0:T(8,128)}), f32[128,128]{1,0:T(8,128)}) %reduce-scatter.2.cloned.1.call-update) | async-done | bytes 65552 | tf_op jit(solution)/shard_map/reduce_scatter | solution.py:80
  (137 shorter events, 51.4 us)
Async XLA Ops:
  7.2 15.7 %copy-start = (bf16[128,8192]{1,0:T(8,128)(2,1)S(1)}, bf16[128,8192]{1,0:T(8,128)(2,1)}, u32[]{:S(2)}) copy-start(bf16[128,8192]{1,0:T(8,128)(2,1)} %param.9) | copy-start | bytes 6291460
  11.1 64.5 %all-to-all-start = ((bf16[128,128,128]{2,1,0:T(8,128)(2,1)}), bf16[128,128,128]{2,1,0:T(8,128)(2,1)}, u32[]{:S(2)}, u32[]{:S(2)}) async-start(bf16[128,128,128]{2,1,0:T(8,128)(2,1)} %stack.2), calls=%async_computation | async-start | bytes 8388608 | tf_op jit(solution)/shard_map/all_to_all | solution.py:44
  22.8 223.9 %all-gather.2.cloned.1.call-start = ((), (), s32[]{:S(2)}) async-start(), calls=%async_computation.2 | async-start | bytes 4227072 | tf_op jit(solution)/shard_map/all_gather | solution.py:49
  25.8 949.8 %reduce-scatter.2.cloned.1.call-start = ((), (), s32[]{:S(2)}) async-start(), calls=%async_computation.3 | async-start | bytes 8454144 | tf_op jit(solution)/shard_map/reduce_scatter | solution.py:80
  25.9 49.7 %copy-start.1 = (bf16[128,512]{1,0:T(8,128)(2,1)S(1)}, bf16[128,512]{1,0:T(8,128)(2,1)}, u32[]{:S(2)}) copy-start(bf16[128,512]{1,0:T(8,128)(2,1)} %param.12) | copy-start | bytes 393220
Sparse Core Ops, SparseCore 0:
  25.9 220.7 all-gather.1
  312.8 662.6 reduce-scatter.1

commit v2 on v0

--- a/solution.py
+++ b/solution.py
@@ -41,7 +41,12 @@
     b_proj = jnp.dot(hidden_states, w_b, preferred_element_type=jnp.float32).astype(jnp.bfloat16)
     key_rows, b_rows = (
         lax.all_gather(teacher_k, ("row", "col"), axis=0, tiled=True),
-        lax.all_gather(b_proj, ("row", "col"), axis=0, tiled=True),
+        jnp.concatenate(
+            lax.all_to_all(
+                jnp.stack([b_proj] * lax.axis_size(("row", "col"))), ("row", "col"), 0, 0
+            ),
+            axis=0,
+        ),
     )
     total_keys = key_rows.shape[0]
     width = math.gcd(2048, total_keys)

time: 1150 us -> 1040 us (0.904)
  waiting for transfers between devices: 994 us -> 873 us
  starting transfers between devices: 0.12 us -> 11.8 us
    all_gather x1 -> x0, waiting for transfers between devices: 139 us -> none  [on_device(): lax.all_gather(b_proj, ('row', 'col'), axis=0, tiled=True)]
    all_gather x1, waiting for transfers between devices: 193 us -> 212 us  [on_device(): lax.all_gather(teacher_k, ('row', 'col'), axis=0, tiled=True)]
    all_to_all x0 -> x1, starting transfers between devices: none -> 11.7 us  [on_device(): lax.all_to_all(jnp.stack([b_proj] * lax.axis_size(('row', 'col'))), ('row...]
  transfers between devices with their start and end apart: 3 -> 3, of which waited for: 3 -> 2; matrix products, arithmetic and copies ran while one was open for 6% -> 7% of each run, Pallas kernels for 0% -> 0%
where the time goes in v2:
time: 1040 us
  waiting for transfers between devices  873 us (84%)
  matrix products  98.9 us (10%)
  other arithmetic  34.2 us (3%)
  between operations  14.1 us (1%)
  starting transfers between devices  11.8 us (1%)
    reduce_scatter x1, waiting for transfers between devices, on_device(): lax.psum_scatter(key_stack.reshape(total_keys, HEAD), ('row', 'col'), sca...  660 us
    all_gather x1, waiting for transfers between devices, on_device(): lax.all_gather(teacher_k, ('row', 'col'), axis=0, tiled=True)  212 us
    dot_general x16, matrix products, teacher_logits(): jnp.einsum('qhp,kp->hqk', shaped, key_rows, preferred_element_type=jnp.fl...  52.2 us
    reduce_sum x8, other arithmetic, stats_step(): jnp.sum(jnp.where(visible, jnp.exp(logits - newest[:, :, None]), 0.0), ax...  25.8 us
  transfers between devices with their start and end apart: 3, of which 2 were waited for; matrix products, arithmetic and copies ran while one was open for 7% of the time, Pallas kernels for 0%

profile of v2, /device:TPU:0, one launch (start us, length us, event | category | flops | bytes accessed | tf_op | source)
XLA Modules:
  0.0 1037.5 jit_solution(8084593693383737608)
XLA Ops:
  8.8 2.3 convolution_convert_fusion.1
  11.1 3.0 stack.2
  14.0 11.7 %all-to-all-start = ((bf16[128,128,128]{2,1,0:T(8,128)(2,1)}), bf16[128,128,128]{2,1,0:T(8,128)(2,1)}, u32[]{:S(2)}, u32[]{:S(2)}) async-start(bf16[128,128,128]{2,1,0:T(8,128)(2,1)} %stack.2), calls=%async_computation | async-start | bytes 8388608 | tf_op jit(solution)/shard_map/all_to_all | solution.py:45
  25.9 4.7 convolution_convert_fusion
  30.6 212.3 %all-gather.2.cloned.1.call-done = bf16[16384,128]{1,0:T(8,128)(2,1)} async-done(((bf16[128,128]{1,0:T(8,128)(2,1)}), bf16[16384,128]{1,0:T(8,128)(2,1)}) %all-gather.2.cloned.1.call-update) | async-done | bytes 4194320 | tf_op jit(solution)/shard_map/all_gather | solution.py:43
  242.9 59.1 %while.33 = (s32[]{:T(128)}, f32[4,128]{1,0:T(4,128)S(1)}, f32[4,128]{1,0:T(4,128)S(1)}, s32[8,2048]{1,0:T(8,128)S(1)}, bf16[8,2048,128]{2,1,0:T(8,128)(2,1)}, /...) while((s32[]{:T(128)}, f32[4,128]{1,0:T(4,128)S(1)}, ...), condition=%wide.region_3.4_spmd.clone.clone.clone, body=%wide.region_0.3_spmd.clone.clone.clone.sunk | while | flops 277089408 | bytes 9884788 | solution.py:70
  243.2 3.7 fusion.81
  247.0 3.2 select_reduce_fusion.2
  250.6 3.7 fusion.81
  254.4 3.2 select_reduce_fusion.2
  258.0 3.7 fusion.81
  261.8 3.2 select_reduce_fusion.2
  265.4 3.7 fusion.81
  269.2 3.2 select_reduce_fusion.2
  272.8 3.7 fusion.81
  276.6 3.2 select_reduce_fusion.2
  280.2 3.7 fusion.81
  283.9 3.2 select_reduce_fusion.2
  287.6 3.7 fusion.81
  291.3 3.2 select_reduce_fusion.2
  295.0 3.7 fusion.81
  298.7 3.2 select_reduce_fusion.2
  302.0 66.0 %while.34 = (s32[]{:T(128)}, f32[128,512]{0,1:T(8,128)S(1)}, f32[8,2048,128]{2,1,0:T(8,128)}, bf16[8,2048,128]{2,1,0:T(8,128)(2,1)}, s32[8,2048]{1,0:T(8,128)S(1...) while((s32[]{:T(128)}, f32[128,512]{0,1:T(8,128)S(1)}, ...), condition=%wide.region_5.6_spmd.clone.clone.clone, body=%wide.region_4.5_spmd.clone.clone.clone.sunk | while | flops 1083573120 | bytes 19301524 | solution.py:77
  304.1 2.8 fusion.96
  312.4 2.8 fusion.96
  320.7 2.8 fusion.96
  328.9 2.8 fusion.96
  337.2 2.8 fusion.96
  345.4 2.8 fusion.96
  353.7 2.8 fusion.96
  361.9 2.8 fusion.96
  368.9 660.3 %reduce-scatter.2.cloned.1.call-done = f32[128,128]{1,0:T(8,128)} async-done(((f32[16384,128]{1,0:T(8,128)}), f32[128,128]{1,0:T(8,128)}) %reduce-scatter.2.cloned.1.call-update) | async-done | bytes 65552 | tf_op jit(solution)/shard_map/reduce_scatter | solution.py:80
  (137 shorter events, 50.1 us)
Async XLA Ops:
  7.2 1.6 copy-start
  7.2 235.7 %all-gather.2.cloned.1.call-start = ((), (), s32[]{:S(2)}) async-start(), calls=%async_computation.2 | async-start | bytes 4227072 | tf_op jit(solution)/shard_map/all_gather | solution.py:43
  14.0 288.0 %all-to-all-start = ((bf16[128,128,128]{2,1,0:T(8,128)(2,1)}), bf16[128,128,128]{2,1,0:T(8,128)(2,1)}, u32[]{:S(2)}, u32[]{:S(2)}) async-start(bf16[128,128,128]{2,1,0:T(8,128)(2,1)} %stack.2), calls=%async_computation | async-start | bytes 8388608 | tf_op jit(solution)/shard_map/all_to_all | solution.py:45
  25.7 1003.5 %reduce-scatter.2.cloned.1.call-start = ((), (), s32[]{:S(2)}) async-start(), calls=%async_computation.3 | async-start | bytes 8454144 | tf_op jit(solution)/shard_map/reduce_scatter | solution.py:80
  25.9 217.0 %copy-start.1 = (bf16[128,512]{1,0:T(8,128)(2,1)S(1)}, bf16[128,512]{1,0:T(8,128)(2,1)}, u32[]{:S(2)}) copy-start(bf16[128,512]{1,0:T(8,128)(2,1)} %param.12) | copy-start | bytes 393220
Sparse Core Ops, SparseCore 0:
  9.7 233.0 all-gather.1
  368.2 660.9 reduce-scatter.1
